TPU v7x, 32 devices: a whole 2x2x4 slice. The times are simulated.
32 devices in a mesh: row: 4 (over x, core), col: 8 (over z, y).
Axes of the slice: x: 2, y: 2, z: 4, core: 2. Of those that a mesh axis runs over, the one named last changes fastest.
Arguments:
- tensor: float32 [1024, 32, 1024], P(None, 'row', 'col'), may hold values from -60 to 60, as said below
- factor_two: float32 [32, 32], P('row'), may hold values from -1 to 1
- factor_three: float32 [32, 32], P('col'), may hold values from -1 to 1
- factor_four: float32 [32, 16], replicated, may hold values from -1 to 1
- factor_init: float32 [1024, 64], replicated, may hold values from -6 to 6
Outputs:
- factor_new: float32 [1024, 64], replicated
- core: float32 [64, 32, 32, 16], P(None, 'row', 'col')
Inputs may be any that keep to these rules, and one draw needn't show every extreme that they name: `tensor`: scales vary from slab to slab.
All inputs are finite; a program needn't handle non-finite values.
Results may differ from a plain program's by a relative error of at most 0.00013.
Values sent between devices are 32-bit elements; how exact they have to be, the bound alone decides.
A program may use at most 128 MiB of HBM per device.

v0:
```python
import jax
import jax.numpy as jnp
from jax import lax
from jax.sharding import PartitionSpec as P


def shards(tensor, factor_two, factor_three, factor_four, factor_init):
    highest = lax.Precision.HIGHEST
    first_len = tensor.shape[0]
    local_two = tensor.shape[1]
    fourth_len = factor_four.shape[0]
    local_three = tensor.shape[2] // fourth_len
    rank_one = factor_init.shape[1]
    data = tensor.reshape(first_len, local_two, local_three, fourth_len)
    fourth = jnp.einsum("abcd,de->abce", data, factor_four, precision=highest)
    whole_two = lax.all_gather(factor_two, "row", axis=0, tiled=True)
    spread_two = lax.all_to_all(fourth, "row", split_axis=0, concat_axis=1, tiled=True)
    projected_two = jnp.einsum("abce,bg->agce", spread_two, whole_two, precision=highest)
    partial_two = lax.all_to_all(projected_two, "row", split_axis=1, concat_axis=0, tiled=True)
    whole_three = lax.all_gather(factor_three, "col", axis=0, tiled=True)
    spread_three = lax.all_to_all(partial_two, "col", split_axis=0, concat_axis=2, tiled=True)
    projected_three = jnp.einsum("agce,cf->agfe", spread_three, whole_three, precision=highest)
    block = lax.all_to_all(projected_three, "col", split_axis=2, concat_axis=0, tiled=True)
    columns = block.reshape(first_len, -1)
    basis = factor_init
    local_gram = jnp.dot(columns, columns.T, precision=highest, preferred_element_type=jnp.float32)
    gram = lax.psum(local_gram, ("row", "col"))
    image = jnp.dot(gram, basis, precision=highest, preferred_element_type=jnp.float32)
    square = jnp.dot(image.T, image, precision=highest, preferred_element_type=jnp.float32)
    lower = jnp.linalg.cholesky(square)
    basis = jax.scipy.linalg.solve_triangular(lower, image.T, lower=True).T
    core = jnp.dot(basis.T, columns, precision=highest, preferred_element_type=jnp.float32)
    return (basis, core.reshape(rank_one, block.shape[1], block.shape[2], block.shape[3]))


def solution(mesh):
    in_specs = (P(None, "row", "col"), P("row", None), P("col", None), P(), P())
    out_specs = (P(), P(None, "row", "col", None))
    return jax.shard_map(shards, mesh=mesh, in_specs=in_specs, out_specs=out_specs, check_vma=False)
```

profile of v0, /device:TPU:0, one launch (start us, length us, event | category | flops | bytes accessed | tf_op | source)
XLA Modules:
  0.0 512.5 jit_solution(1816454857235836736)
XLA Ops:
  7.2 0.0 copy-start
  7.2 0.0 copy-start.4
  7.2 5.5 %copy.18 = f32[1024,8,128]{0,2,1:T(8,128)} copy(f32[1024,8,128]{2,1,0:T(8,128)} %param.5) | data formatting | bytes 8388608 | tf_op args[0]
  12.6 0.0 copy-done.4
  12.6 4.2 fusion.12
  16.8 12.2 %copy.19 = f32[1024,8,4,16]{3,2,1,0:T(4,128)} copy(f32[1024,8,4,16]{0,3,2,1:T(8,128)S(1)} %fusion.12) | data formatting | bytes 4194304 | tf_op jit(solution)/shard_map/abcd,de->abce/dot_general | solution.py:15
  29.0 15.5 %reshape.31 = f32[4,1,131072]{2,1,0:T(1,128)} reshape(f32[1024,8,4,16]{3,2,1,0:T(4,128)} %copy.19) | data formatting | bytes 4194304
  44.5 4.4 all-to-all-start
  48.9 26.7 %all_gather.6 = f32[32,32]{1,0:T(8,128)S(1)} all-gather(f32[8,32]{1,0:T(8,128)S(1)} %copy-done.5), channel_id=1, replica_groups=mesh['row'=4,'col'=8] {'row'}, dimensions={0}, use_global_device_ids=true | all-gather | bytes 5120 | tf_op jit(solution)/shard_map/all_gather | solution.py:16
  75.5 0.0 all-to-all-done
  75.5 1.4 copy-done.2
  76.9 0.5 broadcast.53
  77.4 7.7 %reduce.6 = f32[4,131072]{1,0:T(4,128)S(1)} reduce(f32[4,1,131072]{2,1,0:T(1,128)} %copy-done.2, f32[]{:T(128)} %broadcast.53), dimensions={1}, to_apply=%all_to_all.50.reduce_sub_computation | reduce | bytes 4194308 | tf_op jit(solution)/shard_map/all_to_all | solution.py:17
  85.1 17.9 %reshape.32 = f32[1024,8,4,16]{3,2,1,0:T(4,128)} reshape(f32[4,131072]{1,0:T(4,128)S(1)} %reduce.6) | data formatting | bytes 4194304
  103.0 12.2 %copy.20 = f32[4,256,8,4,16]{1,2,0,4,3:T(8,128)S(1)} copy(f32[4,256,8,4,16]{4,3,2,1,0:T(4,128)} %bitcast.72) | data formatting | bytes 4194304 | tf_op jit(solution)/shard_map/all_to_all | solution.py:17
  115.3 1.9 fusion.2
  117.2 1.2 copy.21
  118.4 28.1 %all_to_all.69 = f32[256,32,4,16]{0,3,2,1:T(8,128)S(1)} all-to-all(f32[256,32,4,16]{0,3,2,1:T(8,128)S(1)} %copy.21), channel_id=1, replica_groups=mesh['row'=4,'col'=8] {'row'}, dimensions={1} | all-to-all | bytes 4194304 | tf_op jit(solution)/shard_map/all_to_all | solution.py:19
  146.6 12.1 %copy.37 = f32[256,4,8,4,16]{4,3,2,0,1:T(4,128)} copy(f32[256,4,8,4,16]{0,4,3,2,1:T(8,128)S(1)} %bitcast.78) | data formatting | bytes 4194304 | tf_op jit(solution)/shard_map/all_to_all | solution.py:19
  158.6 15.4 %reshape.33 = f32[8,1,65536]{2,1,0:T(1,128)} reshape(f32[1024,8,4,16]{3,2,1,0:T(4,128)} %bitcast.73) | data formatting | bytes 4194304
  174.0 6.8 %all-to-all-start.2 = ((f32[8,1,65536]{2,1,0:T(1,128)}), f32[8,1,65536]{2,1,0:T(1,128)}, u32[]{:S(2)}, u32[]{:S(2)}) async-start(f32[8,1,65536]{2,1,0:T(1,128)} %reshape.33), calls=%async_computation.2 | async-start | bytes 4194304 | tf_op jit(solution)/shard_map/all_to_all | solution.py:21
  180.8 0.0 all-reduce.2.cloned.1.call-start
  180.9 66.5 %all-gather = f32[8,4,32]{2,1,0:T(4,128)S(1)} all-gather(f32[1,4,32]{2,1,0:T(4,128)S(1)} %bitcast.85), channel_id=1, replica_groups=mesh['row'=4,'col'=8] {'col'}, dimensions={0}, use_global_device_ids=true | all-gather | bytes 4608 | tf_op jit(solution)/shard_map/all_gather | solution.py:20
  247.3 0.0 all-to-all-done.2
  247.3 7.2 %reduce.7 = f32[8,65536]{1,0:T(8,128)S(1)} reduce(f32[8,1,65536]{2,1,0:T(1,128)} %all-to-all-done.2, f32[]{:T(128)} %broadcast.53), dimensions={1}, to_apply=%all_to_all.58.reduce_sub_computation | reduce | bytes 4194308 | tf_op jit(solution)/shard_map/all_to_all | solution.py:21
  254.6 17.3 %reshape.34 = f32[1024,8,4,16]{3,2,1,0:T(4,128)} reshape(f32[8,65536]{1,0:T(8,128)S(1)} %reduce.7) | data formatting | bytes 4194304
  271.9 9.8 %copy.35 = f32[8,128,8,4,16]{1,0,4,3,2:T(8,128)S(1)} copy(f32[8,128,8,4,16]{4,3,2,1,0:T(4,128)} %bitcast.74) | data formatting | bytes 4194304 | tf_op jit(solution)/shard_map/all_to_all | solution.py:21
  281.7 1.4 copy.25
  283.1 1.9 convolution_bitcast_fusion
  285.0 1.2 copy.27
  286.2 46.2 %all_to_all.70 = f32[128,8,32,16]{0,3,1,2:T(8,128)S(1)} all-to-all(f32[128,8,32,16]{0,3,1,2:T(8,128)S(1)} %copy.27), channel_id=1, replica_groups=mesh['row'=4,'col'=8] {'col'}, dimensions={2} | all-to-all | bytes 4194304 | tf_op jit(solution)/shard_map/all_to_all | solution.py:23
  332.5 1.2 copy.28
  333.7 8.9 %fusion.14 = f32[1024,1024]{1,0:T(8,128)} fusion(f32[64,8,8,128]{3,2,1,0:T(8,128)S(1)} %bitcast.75), kind=kOutput, calls=%fused_computation.20 | convolution fusion | flops 6442450944 | bytes 6291456 | tf_op jit(solution)/shard_map/dot_general | solution.py:26
  342.6 0.0 all-reduce.2.cloned.1.call-update
  342.7 1.9 copy.41
  344.5 138.8 %all-reduce.2.cloned.1.call-done = f32[1024,1024]{1,0:T(8,128)} async-done(((f32[1024,1024]{1,0:T(8,128)}), f32[1024,1024]{1,0:T(8,128)}) %all-reduce.2.cloned.1.call-update) | async-done | bytes 4194320 | tf_op jit(solution)/shard_map/psum | solution.py:27
  483.4 6.3 %fusion.15 = f32[1024,64]{0,1:T(8,128)S(1)} fusion(f32[1024,1024]{1,0:T(8,128)} %all-reduce.2.cloned.1.call-done, f32[1024,64]{0,1:T(8,128)S(1)} %copy-done), kind=kOutput, calls=%fused_computation.21 | convolution fusion | flops 805306368 | bytes 4718592 | tf_op jit(solution)/shard_map/dot_general | solution.py:28
  489.7 0.4 fusion.16
  490.1 0.1 copy.29
  490.2 5.8 %cholesky.16 = f32[64,64]{1,0:T(8,128)S(1)} custom-call(f32[64,64]{1,0:T(8,128)S(1)} %fusion.10), custom_call_target="Cholesky" | custom-call | tf_op jit(solution)/shard_map/jit(cholesky)/cholesky | solution.py:30
  496.0 0.6 compare_reduce_fusion
  496.7 0.7 fusion.7
  497.3 4.9 custom-call.7
  502.2 0.4 fusion.8
  502.7 0.0 copy-start.3
  502.7 0.0 copy-done.1
  502.7 2.5 fusion.5
  505.2 0.0 copy-done.3
  (9 shorter events, 0.1 us)
Async XLA Ops:
  7.2 476.2 %copy-start = (f32[1024,64]{0,1:T(8,128)S(1)}, f32[1024,64]{0,1:T(8,128)}, u32[]{:S(2)}) copy-start(f32[1024,64]{0,1:T(8,128)} %param.9) | copy-start | bytes 786436
  7.2 5.5 %copy-start.4 = (f32[32,16]{0,1:T(8,128)S(1)}, f32[32,16]{0,1:T(8,128)}, u32[]{:S(2)}) copy-start(f32[32,16]{0,1:T(8,128)} %param.8) | copy-start | bytes 6148
  44.5 4.4 copy-start.5
  44.5 31.1 %all-to-all-start = ((f32[4,1,131072]{2,1,0:T(1,128)}), f32[4,1,131072]{2,1,0:T(1,128)S(1)}, u32[]{:S(2)}, u32[]{:S(2)}) async-start(f32[4,1,131072]{2,1,0:T(1,128)} %reshape.31), calls=%async_computation | async-start | bytes 4194304 | tf_op jit(solution)/shard_map/all_to_all | solution.py:17
  75.5 1.4 copy-start.2
  174.0 6.8 %copy-start.6 = (f32[4,32]{1,0:T(4,128)S(1)}, f32[4,32]{1,0:T(4,128)}, u32[]{:S(2)}) copy-start(f32[4,32]{1,0:T(4,128)} %param.7) | copy-start | bytes 1540
  174.0 73.3 %all-to-all-start.2 = ((f32[8,1,65536]{2,1,0:T(1,128)}), f32[8,1,65536]{2,1,0:T(1,128)}, u32[]{:S(2)}, u32[]{:S(2)}) async-start(f32[8,1,65536]{2,1,0:T(1,128)} %reshape.33), calls=%async_computation.2 | async-start | bytes 4194304 | tf_op jit(solution)/shard_map/all_to_all | solution.py:21
  180.8 302.5 %all-reduce.2.cloned.1.call-start = ((), (), s32[]{:S(2)}) async-start(), calls=%async_computation.4 | async-start | bytes 8388608 | tf_op jit(solution)/shard_map/psum | solution.py:27
  344.5 158.2 %copy-start.1 = (f32[64,8,8,128]{3,1,2,0:T(8,128)S(1)}, f32[64,8,8,128]{3,1,2,0:T(8,128)}, u32[]{:S(2)}) copy-start(f32[64,8,8,128]{3,1,2,0:T(8,128)} %copy.41) | copy-start | bytes 6291460
  502.7 2.5 copy-start.3
Sparse Core Ops, SparseCore 0:
  342.8 140.5 all-reduce.1
where the time goes:
time: 518 us; the launch traced here: 512 us
  blocking collectives  168 us (32%)
  waiting for transfers between devices  139 us (27%)
  local copies, waits for them, and re-layouts  127 us (25%)
  other arithmetic  27 us (5%)
  matrix products  26.5 us (5%)
  between operations  14.6 us (3%)
  starting transfers between devices  11.2 us (2%)
    psum x1, waiting for transfers between devices, shards(): gram = lax.psum(local_gram, ('row', 'col'))  139 us
    unnamed x20, local copies, waits for them, and re-layouts  74.8 us
    all_gather x1, blocking collectives, shards(): whole_three = lax.all_gather(factor_three, 'col', axis=0, tiled=True)  66.5 us
    all_to_all x1, blocking collectives, shards(): lax.all_to_all(projected_three, 'col', split_axis=2, concat_axis=0, tiled...  46.2 us
    all_to_all x1, blocking collectives, shards(): lax.all_to_all(projected_two, 'row', split_axis=1, concat_axis=0, tiled=T...  28.1 us
    all_gather x1, blocking collectives, shards(): whole_two = lax.all_gather(factor_two, 'row', axis=0, tiled=True)  26.7 us
    all_to_all x2, local copies, waits for them, and re-layouts, shards(): lax.all_to_all(fourth, 'row', split_axis=0, concat_axis=1, tiled=True)  12.7 us
    dot_general x1, local copies, waits for them, and re-layouts, shards(): fourth = jnp.einsum('abcd,de->abce', data, factor_four, precision=highest)  12.2 us
  transfers between devices with their start and end apart: 3, of which 1 were waited for; matrix products, arithmetic and copies ran while one was open for 0% of the time, Pallas kernels for 0%

commit v1 on v0

--- a/solution.py
+++ b/solution.py
@@ -24,7 +24,7 @@
     columns = block.reshape(first_len, -1)
     basis = factor_init
     local_gram = jnp.dot(columns, columns.T, precision=highest, preferred_element_type=jnp.float32)
-    gram = lax.psum(local_gram, ("row", "col"))
+    gram = lax.psum(lax.psum(local_gram, "row"), "col")
     image = jnp.dot(gram, basis, precision=highest, preferred_element_type=jnp.float32)
     square = jnp.dot(image.T, image, precision=highest, preferred_element_type=jnp.float32)
     lower = jnp.linalg.cholesky(square)

time: 518 us -> 621 us (1.20)
  waiting for transfers between devices: 139 us -> 242 us
    psum x1 -> x2, waiting for transfers between devices: 139 us -> 242 us  [shards(): gram = lax.psum(lax.psum(local_gram, 'row'), 'col')]
  transfers between devices with their start and end apart: 3 -> 4, of which waited for: 1 -> 2; matrix products, arithmetic and copies ran while one was open for 0% -> 0% of each run, Pallas kernels for 0% -> 0%
where the time goes in v1:
time: 621 us; the launch traced here: 616 us
  waiting for transfers between devices  242 us (39%)
  blocking collectives  168 us (27%)
  local copies, waits for them, and re-layouts  127 us (20%)
  other arithmetic  27 us (4%)
  matrix products  26.3 us (4%)
  between operations  14.6 us (2%)
  starting transfers between devices  11.5 us (2%)
    psum x2, waiting for transfers between devices, shards(): gram = lax.psum(lax.psum(local_gram, 'row'), 'col')  242 us
    unnamed x20, local copies, waits for them, and re-layouts  74.8 us
    all_gather x1, blocking collectives, shards(): whole_three = lax.all_gather(factor_three, 'col', axis=0, tiled=True)  66.5 us
    all_to_all x1, blocking collectives, shards(): lax.all_to_all(projected_three, 'col', split_axis=2, concat_axis=0, tiled...  46.2 us
    all_to_all x1, blocking collectives, shards(): lax.all_to_all(projected_two, 'row', split_axis=1, concat_axis=0, tiled=T...  28.1 us
    all_gather x1, blocking collectives, shards(): whole_two = lax.all_gather(factor_two, 'row', axis=0, tiled=True)  26.7 us
    all_to_all x2, local copies, waits for them, and re-layouts, shards(): lax.all_to_all(fourth, 'row', split_axis=0, concat_axis=1, tiled=True)  12.7 us
  transfers between devices with their start and end apart: 4, of which 2 were waited for; matrix products, arithmetic and copies ran while one was open for 0% of the time, Pallas kernels for 0%

profile of v1, /device:TPU:0, one launch (start us, length us, event | category | flops | bytes accessed | tf_op | source)
XLA Modules:
  0.0 615.7 jit_solution(13689654708125370836)
XLA Ops:
  7.2 0.0 copy-start
  7.2 5.5 copy.18
  12.6 0.0 copy-done.4
  12.6 4.2 fusion.12
  16.8 12.2 %copy.19 = f32[1024,8,4,16]{3,2,1,0:T(4,128)} copy(f32[1024,8,4,16]{0,3,2,1:T(8,128)S(1)} %fusion.12) | data formatting | bytes 4194304 | tf_op jit(solution)/shard_map/abcd,de->abce/dot_general | solution.py:15
  29.0 15.5 %reshape.31 = f32[4,1,131072]{2,1,0:T(1,128)} reshape(f32[1024,8,4,16]{3,2,1,0:T(4,128)} %copy.19) | data formatting | bytes 4194304
  44.5 4.4 all-to-all-start
  48.9 26.7 %all_gather.6 = f32[32,32]{1,0:T(8,128)S(1)} all-gather(f32[8,32]{1,0:T(8,128)S(1)} %copy-done.5), channel_id=1, replica_groups=mesh['row'=4,'col'=8] {'row'}, dimensions={0}, use_global_device_ids=true | all-gather | bytes 5120 | tf_op jit(solution)/shard_map/all_gather | solution.py:16
  75.5 0.0 all-to-all-done
  75.5 1.4 copy-done.2
  76.9 0.5 broadcast.53
  77.4 7.7 %reduce.6 = f32[4,131072]{1,0:T(4,128)S(1)} reduce(f32[4,1,131072]{2,1,0:T(1,128)} %copy-done.2, f32[]{:T(128)} %broadcast.53), dimensions={1}, to_apply=%all_to_all.50.reduce_sub_computation | reduce | bytes 4194308 | tf_op jit(solution)/shard_map/all_to_all | solution.py:17
  85.1 17.9 %reshape.32 = f32[1024,8,4,16]{3,2,1,0:T(4,128)} reshape(f32[4,131072]{1,0:T(4,128)S(1)} %reduce.6) | data formatting | bytes 4194304
  103.0 12.2 %copy.20 = f32[4,256,8,4,16]{1,2,0,4,3:T(8,128)S(1)} copy(f32[4,256,8,4,16]{4,3,2,1,0:T(4,128)} %bitcast.72) | data formatting | bytes 4194304 | tf_op jit(solution)/shard_map/all_to_all | solution.py:17
  115.3 1.9 fusion.2
  117.2 1.2 copy.21
  118.4 28.1 %all_to_all.69 = f32[256,32,4,16]{0,3,2,1:T(8,128)S(1)} all-to-all(f32[256,32,4,16]{0,3,2,1:T(8,128)S(1)} %copy.21), channel_id=1, replica_groups=mesh['row'=4,'col'=8] {'row'}, dimensions={1} | all-to-all | bytes 4194304 | tf_op jit(solution)/shard_map/all_to_all | solution.py:19
  146.6 12.1 %copy.37 = f32[256,4,8,4,16]{4,3,2,0,1:T(4,128)} copy(f32[256,4,8,4,16]{0,4,3,2,1:T(8,128)S(1)} %bitcast.78) | data formatting | bytes 4194304 | tf_op jit(solution)/shard_map/all_to_all | solution.py:19
  158.6 15.4 %reshape.33 = f32[8,1,65536]{2,1,0:T(1,128)} reshape(f32[1024,8,4,16]{3,2,1,0:T(4,128)} %bitcast.73) | data formatting | bytes 4194304
  174.0 6.8 %all-to-all-start.2 = ((f32[8,1,65536]{2,1,0:T(1,128)}), f32[8,1,65536]{2,1,0:T(1,128)}, u32[]{:S(2)}, u32[]{:S(2)}) async-start(f32[8,1,65536]{2,1,0:T(1,128)} %reshape.33), calls=%async_computation.2 | async-start | bytes 4194304 | tf_op jit(solution)/shard_map/all_to_all | solution.py:21
  180.8 0.0 all-reduce.3.cloned.1.call-start
  180.9 66.5 %all-gather = f32[8,4,32]{2,1,0:T(4,128)S(1)} all-gather(f32[1,4,32]{2,1,0:T(4,128)S(1)} %bitcast.85), channel_id=1, replica_groups=mesh['row'=4,'col'=8] {'col'}, dimensions={0}, use_global_device_ids=true | all-gather | bytes 4608 | tf_op jit(solution)/shard_map/all_gather | solution.py:20
  247.3 0.0 all-to-all-done.2
  247.3 7.2 %reduce.7 = f32[8,65536]{1,0:T(8,128)S(1)} reduce(f32[8,1,65536]{2,1,0:T(1,128)} %all-to-all-done.2, f32[]{:T(128)} %broadcast.53), dimensions={1}, to_apply=%all_to_all.58.reduce_sub_computation | reduce | bytes 4194308 | tf_op jit(solution)/shard_map/all_to_all | solution.py:21
  254.6 17.3 %reshape.34 = f32[1024,8,4,16]{3,2,1,0:T(4,128)} reshape(f32[8,65536]{1,0:T(8,128)S(1)} %reduce.7) | data formatting | bytes 4194304
  271.9 9.8 %copy.35 = f32[8,128,8,4,16]{1,0,4,3,2:T(8,128)S(1)} copy(f32[8,128,8,4,16]{4,3,2,1,0:T(4,128)} %bitcast.74) | data formatting | bytes 4194304 | tf_op jit(solution)/shard_map/all_to_all | solution.py:21
  281.7 1.4 copy.25
  283.1 1.9 convolution_bitcast_fusion
  285.0 1.2 copy.27
  286.2 46.2 %all_to_all.70 = f32[128,8,32,16]{0,3,1,2:T(8,128)S(1)} all-to-all(f32[128,8,32,16]{0,3,1,2:T(8,128)S(1)} %copy.27), channel_id=1, replica_groups=mesh['row'=4,'col'=8] {'col'}, dimensions={2} | all-to-all | bytes 4194304 | tf_op jit(solution)/shard_map/all_to_all | solution.py:23
  332.5 1.2 copy.28
  333.7 8.7 %fusion.14 = f32[1024,1024]{1,0:T(8,128)} fusion(f32[64,8,8,128]{3,2,1,0:T(8,128)S(1)} %bitcast.75), kind=kOutput, calls=%fused_computation.20 | convolution fusion | flops 6442450944 | bytes 6291456 | tf_op jit(solution)/shard_map/dot_general | solution.py:26
  342.4 0.0 all-reduce.3.cloned.1.call-update
  342.4 0.3 all-reduce.5.cloned.1.call-start
  342.7 83.6 %all-reduce.3.cloned.1.call-done = f32[1024,1024]{1,0:T(8,128)} async-done(((f32[1024,1024]{1,0:T(8,128)}), f32[1024,1024]{1,0:T(8,128)}) %all-reduce.3.cloned.1.call-update) | async-done | bytes 4194320 | tf_op jit(solution)/shard_map/psum | solution.py:27
  426.3 0.0 all-reduce.5.cloned.1.call-update
  426.4 1.9 copy.41
  428.2 158.4 %all-reduce.5.cloned.1.call-done = f32[1024,1024]{1,0:T(8,128)} async-done(((f32[1024,1024]{1,0:T(8,128)}), f32[1024,1024]{1,0:T(8,128)}) %all-reduce.5.cloned.1.call-update) | async-done | bytes 4194320 | tf_op jit(solution)/shard_map/psum | solution.py:27
  586.6 6.3 %fusion.15 = f32[1024,64]{0,1:T(8,128)S(1)} fusion(f32[1024,1024]{1,0:T(8,128)} %all-reduce.5.cloned.1.call-done, f32[1024,64]{0,1:T(8,128)S(1)} %copy-done), kind=kOutput, calls=%fused_computation.21 | convolution fusion | flops 805306368 | bytes 4718592 | tf_op jit(solution)/shard_map/dot_general | solution.py:28
  592.9 0.4 fusion.16
  593.3 0.1 copy.29
  593.4 5.8 cholesky.16
  599.3 0.6 compare_reduce_fusion
  599.9 0.7 fusion.7
  600.6 4.9 custom-call.7
  605.5 0.4 fusion.8
  605.9 0.0 copy-start.3
  605.9 2.5 fusion.5
  (12 shorter events, 0.1 us)
Async XLA Ops:
  7.2 579.4 %copy-start = (f32[1024,64]{0,1:T(8,128)S(1)}, f32[1024,64]{0,1:T(8,128)}, u32[]{:S(2)}) copy-start(f32[1024,64]{0,1:T(8,128)} %param.9) | copy-start | bytes 786436
  7.2 5.5 copy-start.4
  44.5 4.4 copy-start.5
  44.5 31.1 %all-to-all-start = ((f32[4,1,131072]{2,1,0:T(1,128)}), f32[4,1,131072]{2,1,0:T(1,128)S(1)}, u32[]{:S(2)}, u32[]{:S(2)}) async-start(f32[4,1,131072]{2,1,0:T(1,128)} %reshape.31), calls=%async_computation | async-start | bytes 4194304 | tf_op jit(solution)/shard_map/all_to_all | solution.py:17
  75.5 1.4 copy-start.2
  174.0 6.8 %copy-start.6 = (f32[4,32]{1,0:T(4,128)S(1)}, f32[4,32]{1,0:T(4,128)}, u32[]{:S(2)}) copy-start(f32[4,32]{1,0:T(4,128)} %param.7) | copy-start | bytes 1540
  174.0 73.3 %all-to-all-start.2 = ((f32[8,1,65536]{2,1,0:T(1,128)}), f32[8,1,65536]{2,1,0:T(1,128)}, u32[]{:S(2)}, u32[]{:S(2)}) async-start(f32[8,1,65536]{2,1,0:T(1,128)} %reshape.33), calls=%async_computation.2 | async-start | bytes 4194304 | tf_op jit(solution)/shard_map/all_to_all | solution.py:21
  180.8 245.5 %all-reduce.3.cloned.1.call-start = ((), (), s32[]{:S(2)}) async-start(), calls=%async_computation.4 | async-start | bytes 8388608 | tf_op jit(solution)/shard_map/psum | solution.py:27
  342.4 244.2 %all-reduce.5.cloned.1.call-start = ((), (), s32[]{:S(2)}) async-start(), calls=%async_computation.5 | async-start | bytes 8388608 | tf_op jit(solution)/shard_map/psum | solution.py:27
  428.2 177.7 %copy-start.1 = (f32[64,8,8,128]{3,1,2,0:T(8,128)S(1)}, f32[64,8,8,128]{3,1,2,0:T(8,128)}, u32[]{:S(2)}) copy-start(f32[64,8,8,128]{3,1,2,0:T(8,128)} %copy.41) | copy-start | bytes 6291460
  605.9 2.5 copy-start.3
Sparse Core Ops, SparseCore 0:
  342.6 83.7 all-reduce.2
  430.0 156.5 all-reduce.4
